TPU v7x, 128 devices: a whole 4x4x4 slice. The times are simulated.
128 devices in a mesh: tok: 16 (over x, y_lo, core), own: 8 (over z, y_hi).
Axes of the slice: x: 4, y: 4 (y_hi: 2, y_lo: 2; y = y_hi * 2 + y_lo), z: 4, core: 2. Of those that a mesh axis runs over, the one named last changes fastest.
Arguments:
- expert_ids: int32 [5, 8, 1048576], P(None, None, ('tok', 'own')), may hold values from 0 to 383, as said below
- shard_length: int32 [128], P(('tok', 'own')), may hold values from 2048 to 8192
Outputs:
- lift: float32 [4, 384, 384], P(None, 'own')
Inputs may be any that keep to these rules, and one draw needn't show every extreme that they name: For each layer and token slot, expert_ids names 8 different experts.
All inputs are finite; a program needn't handle non-finite values.
Results may differ from a plain program's by a relative error of at most 0.0003.
Values sent between devices are 32-bit elements; how exact they have to be, the bound alone decides.
No kernel may reach another device: no remote copies, remote signals or barrier semaphores. Data moves between devices by JAX's collectives and lax.ppermute only.
A program may use at most 64 MiB of HBM per device.

v0:
```python
import functools

import jax
import jax.numpy as jnp
from jax import lax
from jax.sharding import Mesh
from jax.sharding import PartitionSpec as P

E = 384
TOK_OWN = ("tok_0", "tok_1", "tok_2", "own_0", "own_1")
OWN = ("own_0", "own_1")
TOK = ("tok_0", "tok_1", "tok_2")


def over_axes(shard, axes):
    return functools.reduce(lax.psum, axes, shard)


def sum_by_axis(shard, axes, dim):
    if not axes:
        return shard
    nearer = lax.psum_scatter(shard, axes[0], scatter_dimension=dim, tiled=True)
    return sum_by_axis(nearer, axes[1:], dim)


def total_of_pieces(shard, axis):
    pieces = lax.all_gather(shard, axis)
    return pieces.sum(axis=0)


def shards(expert_ids, shard_length):
    layers, chosen, slots = expert_ids.shape
    block = min(slots, 512 * max(1, slots // 8192))
    steps = slots // block
    experts = E
    limit = shard_length[0]
    columns = lax.broadcasted_iota(jnp.int32, (1, 1, experts), 2)

    def one_block(index, carry):
        counts, tiles = carry
        start = index * block
        piece = lax.dynamic_slice_in_dim(expert_ids, start, block, 2)
        rows = start + lax.broadcasted_iota(jnp.int32, (1, block, 1), 1)
        alive = (rows < limit).astype(jnp.bfloat16)
        hot = jnp.zeros((layers, block, experts), jnp.bfloat16)
        for slot in range(chosen):
            hot = hot + (piece[:, slot, :, None] == columns).astype(jnp.bfloat16)
        hot = hot * alive
        counts = counts + jnp.sum(hot, axis=1, dtype=jnp.float32)
        tiles = tiles + jnp.einsum(
            "ltx,lty->lxy", hot[:-1], hot[1:], preferred_element_type=jnp.float32
        )
        return (counts, tiles)

    begin = (
        jnp.zeros((layers, experts), jnp.float32),
        jnp.zeros((layers - 1, experts, experts), jnp.float32),
    )
    counts, tiles = lax.fori_loop(0, steps, one_block, begin)
    counts, total = (over_axes(counts, TOK_OWN), over_axes(limit.astype(jnp.float32), TOK_OWN))
    owners = lax.axis_size(OWN)
    share = experts // owners
    partial_rows = sum_by_axis(tiles, OWN, 1)
    mine = total_of_pieces(partial_rows, TOK)
    first = lax.dynamic_slice_in_dim(counts[:-1], lax.axis_index(OWN) * share, share, 1)
    product = first[:, :, None] * counts[1:, None, :]
    return mine * total / jnp.maximum(product, 1.0)


def solution(mesh):
    torus = Mesh(mesh.devices.reshape(4, 2, 2, 4, 2), ("tok_0", "tok_1", "tok_2", "own_0", "own_1"))
    in_specs = (P(None, None, TOK_OWN), P(TOK_OWN))
    out_specs = P(None, OWN, None)
    return jax.shard_map(
        shards, mesh=torus, in_specs=in_specs, out_specs=out_specs, check_vma=False
    )
```

profile of v0, /device:TPU:0, one launch (start us, length us, event | category | flops | bytes accessed | tf_op | source)
XLA Modules:
  0.0 304.3 jit_solution(13841878595617887138)
XLA Ops:
  6.5 170.8 %while.17 = (s32[]{:T(128)}, f32[5,384]{1,0:T(8,128)S(1)}, f32[4,384,384]{2,1,0:T(8,128)}, s32[5,8,8192]{2,1,0:T(8,128)}, s32[]{:T(128)}, /*index=5*/s32[]{:T(12...) while((s32[]{:T(128)}, f32[5,384]{1,0:T(8,128)S(1)}, ...), condition=%wide.region_2.0_spmd.clone.clone, body=%wide.region_0.0_spmd.clone.clone.sunk | while | flops 640552320 | bytes 10666322 | solution.py:59
  9.0 4.0 %convert_reduce_fusion.2 = (f32[5,384]{1,0:T(8,128)S(1)}, bf16[5,512,384]{2,1,0:T(8,128)(2,1)S(1)}) fusion(bf16[512]{0:T(512)(128)(2,1)S(1)} %fusion.31, s32[5,512]{1,0:T(8,128)S(1)} %get-tuple-element.281, s32[5,512]{1,0:T(8,128)S(1)} %get-tuple-element.282, s32[5,512]{1,0:T(8,128)S(1)} %get-tuple-element.285, s32[5,512]{1,0:T(8,128)S(1)} %get-tuple-element.286, ...), kind=kLoop, calls=%fused_computation.9.clone.1 | loop fusion | flops 35387520 | bytes 2056704 | tf_op jit(solution)/shard_map/while/body/eval_jaxpr/reduce_sum | solution.py:49
  22.2 4.2 %select_add_fusion.5 = f32[4,384,384]{2,1,0:T(8,128)} fusion(f32[4,384,384]{2,1,0:T(8,128)} %get-tuple-element.315, bf16[5,512,384]{2,1,0:T(8,128)(2,1)S(1)} %get-tuple-element.296, pred[]{:T(512)S(6)} %compare.3), kind=kOutput, calls=%fused_computation.18.clone.1 | convolution fusion | flops 605159424 | bytes 8257537 | tf_op jit(solution)/shard_map/while/body/eval_jaxpr/ltx,lty->lxy/dot_general | solution.py:50
  28.8 4.0 %convert_reduce_fusion.2 = (f32[5,384]{1,0:T(8,128)S(1)}, bf16[5,512,384]{2,1,0:T(8,128)(2,1)S(1)}) fusion(bf16[512]{0:T(512)(128)(2,1)S(1)} %fusion.31, s32[5,512]{1,0:T(8,128)S(1)} %get-tuple-element.281, s32[5,512]{1,0:T(8,128)S(1)} %get-tuple-element.282, s32[5,512]{1,0:T(8,128)S(1)} %get-tuple-element.285, s32[5,512]{1,0:T(8,128)S(1)} %get-tuple-element.286, ...), kind=kLoop, calls=%fused_computation.9.clone.1 | loop fusion | flops 35387520 | bytes 2056704 | tf_op jit(solution)/shard_map/while/body/eval_jaxpr/reduce_sum | solution.py:49
  32.9 4.2 %select_add_fusion.5 = f32[4,384,384]{2,1,0:T(8,128)} fusion(f32[4,384,384]{2,1,0:T(8,128)} %get-tuple-element.315, bf16[5,512,384]{2,1,0:T(8,128)(2,1)S(1)} %get-tuple-element.296, pred[]{:T(512)S(6)} %compare.3), kind=kOutput, calls=%fused_computation.18.clone.1 | convolution fusion | flops 605159424 | bytes 8257537 | tf_op jit(solution)/shard_map/while/body/eval_jaxpr/ltx,lty->lxy/dot_general | solution.py:50
  39.6 4.0 %convert_reduce_fusion.2 = (f32[5,384]{1,0:T(8,128)S(1)}, bf16[5,512,384]{2,1,0:T(8,128)(2,1)S(1)}) fusion(bf16[512]{0:T(512)(128)(2,1)S(1)} %fusion.31, s32[5,512]{1,0:T(8,128)S(1)} %get-tuple-element.281, s32[5,512]{1,0:T(8,128)S(1)} %get-tuple-element.282, s32[5,512]{1,0:T(8,128)S(1)} %get-tuple-element.285, s32[5,512]{1,0:T(8,128)S(1)} %get-tuple-element.286, ...), kind=kLoop, calls=%fused_computation.9.clone.1 | loop fusion | flops 35387520 | bytes 2056704 | tf_op jit(solution)/shard_map/while/body/eval_jaxpr/reduce_sum | solution.py:49
  43.6 4.2 %select_add_fusion.5 = f32[4,384,384]{2,1,0:T(8,128)} fusion(f32[4,384,384]{2,1,0:T(8,128)} %get-tuple-element.315, bf16[5,512,384]{2,1,0:T(8,128)(2,1)S(1)} %get-tuple-element.296, pred[]{:T(512)S(6)} %compare.3), kind=kOutput, calls=%fused_computation.18.clone.1 | convolution fusion | flops 605159424 | bytes 8257537 | tf_op jit(solution)/shard_map/while/body/eval_jaxpr/ltx,lty->lxy/dot_general | solution.py:50
  50.4 4.0 %convert_reduce_fusion.2 = (f32[5,384]{1,0:T(8,128)S(1)}, bf16[5,512,384]{2,1,0:T(8,128)(2,1)S(1)}) fusion(bf16[512]{0:T(512)(128)(2,1)S(1)} %fusion.31, s32[5,512]{1,0:T(8,128)S(1)} %get-tuple-element.281, s32[5,512]{1,0:T(8,128)S(1)} %get-tuple-element.282, s32[5,512]{1,0:T(8,128)S(1)} %get-tuple-element.285, s32[5,512]{1,0:T(8,128)S(1)} %get-tuple-element.286, ...), kind=kLoop, calls=%fused_computation.9.clone.1 | loop fusion | flops 35387520 | bytes 2056704 | tf_op jit(solution)/shard_map/while/body/eval_jaxpr/reduce_sum | solution.py:49
  54.4 4.2 %select_add_fusion.5 = f32[4,384,384]{2,1,0:T(8,128)} fusion(f32[4,384,384]{2,1,0:T(8,128)} %get-tuple-element.315, bf16[5,512,384]{2,1,0:T(8,128)(2,1)S(1)} %get-tuple-element.296, pred[]{:T(512)S(6)} %compare.3), kind=kOutput, calls=%fused_computation.18.clone.1 | convolution fusion | flops 605159424 | bytes 8257537 | tf_op jit(solution)/shard_map/while/body/eval_jaxpr/ltx,lty->lxy/dot_general | solution.py:50
  61.1 4.0 %convert_reduce_fusion.2 = (f32[5,384]{1,0:T(8,128)S(1)}, bf16[5,512,384]{2,1,0:T(8,128)(2,1)S(1)}) fusion(bf16[512]{0:T(512)(128)(2,1)S(1)} %fusion.31, s32[5,512]{1,0:T(8,128)S(1)} %get-tuple-element.281, s32[5,512]{1,0:T(8,128)S(1)} %get-tuple-element.282, s32[5,512]{1,0:T(8,128)S(1)} %get-tuple-element.285, s32[5,512]{1,0:T(8,128)S(1)} %get-tuple-element.286, ...), kind=kLoop, calls=%fused_computation.9.clone.1 | loop fusion | flops 35387520 | bytes 2056704 | tf_op jit(solution)/shard_map/while/body/eval_jaxpr/reduce_sum | solution.py:49
  65.1 4.2 %select_add_fusion.5 = f32[4,384,384]{2,1,0:T(8,128)} fusion(f32[4,384,384]{2,1,0:T(8,128)} %get-tuple-element.315, bf16[5,512,384]{2,1,0:T(8,128)(2,1)S(1)} %get-tuple-element.296, pred[]{:T(512)S(6)} %compare.3), kind=kOutput, calls=%fused_computation.18.clone.1 | convolution fusion | flops 605159424 | bytes 8257537 | tf_op jit(solution)/shard_map/while/body/eval_jaxpr/ltx,lty->lxy/dot_general | solution.py:50
  71.8 4.0 %convert_reduce_fusion.2 = (f32[5,384]{1,0:T(8,128)S(1)}, bf16[5,512,384]{2,1,0:T(8,128)(2,1)S(1)}) fusion(bf16[512]{0:T(512)(128)(2,1)S(1)} %fusion.31, s32[5,512]{1,0:T(8,128)S(1)} %get-tuple-element.281, s32[5,512]{1,0:T(8,128)S(1)} %get-tuple-element.282, s32[5,512]{1,0:T(8,128)S(1)} %get-tuple-element.285, s32[5,512]{1,0:T(8,128)S(1)} %get-tuple-element.286, ...), kind=kLoop, calls=%fused_computation.9.clone.1 | loop fusion | flops 35387520 | bytes 2056704 | tf_op jit(solution)/shard_map/while/body/eval_jaxpr/reduce_sum | solution.py:49
  75.9 4.2 %select_add_fusion.5 = f32[4,384,384]{2,1,0:T(8,128)} fusion(f32[4,384,384]{2,1,0:T(8,128)} %get-tuple-element.315, bf16[5,512,384]{2,1,0:T(8,128)(2,1)S(1)} %get-tuple-element.296, pred[]{:T(512)S(6)} %compare.3), kind=kOutput, calls=%fused_computation.18.clone.1 | convolution fusion | flops 605159424 | bytes 8257537 | tf_op jit(solution)/shard_map/while/body/eval_jaxpr/ltx,lty->lxy/dot_general | solution.py:50
  82.8 4.0 %convert_reduce_fusion.2 = (f32[5,384]{1,0:T(8,128)S(1)}, bf16[5,512,384]{2,1,0:T(8,128)(2,1)S(1)}) fusion(bf16[512]{0:T(512)(128)(2,1)S(1)} %fusion.31, s32[5,512]{1,0:T(8,128)S(1)} %get-tuple-element.281, s32[5,512]{1,0:T(8,128)S(1)} %get-tuple-element.282, s32[5,512]{1,0:T(8,128)S(1)} %get-tuple-element.285, s32[5,512]{1,0:T(8,128)S(1)} %get-tuple-element.286, ...), kind=kLoop, calls=%fused_computation.9.clone.1 | loop fusion | flops 35387520 | bytes 2056704 | tf_op jit(solution)/shard_map/while/body/eval_jaxpr/reduce_sum | solution.py:49
  86.8 4.2 %select_add_fusion.5 = f32[4,384,384]{2,1,0:T(8,128)} fusion(f32[4,384,384]{2,1,0:T(8,128)} %get-tuple-element.315, bf16[5,512,384]{2,1,0:T(8,128)(2,1)S(1)} %get-tuple-element.296, pred[]{:T(512)S(6)} %compare.3), kind=kOutput, calls=%fused_computation.18.clone.1 | convolution fusion | flops 605159424 | bytes 8257537 | tf_op jit(solution)/shard_map/while/body/eval_jaxpr/ltx,lty->lxy/dot_general | solution.py:50
  93.6 4.0 %convert_reduce_fusion.2 = (f32[5,384]{1,0:T(8,128)S(1)}, bf16[5,512,384]{2,1,0:T(8,128)(2,1)S(1)}) fusion(bf16[512]{0:T(512)(128)(2,1)S(1)} %fusion.31, s32[5,512]{1,0:T(8,128)S(1)} %get-tuple-element.281, s32[5,512]{1,0:T(8,128)S(1)} %get-tuple-element.282, s32[5,512]{1,0:T(8,128)S(1)} %get-tuple-element.285, s32[5,512]{1,0:T(8,128)S(1)} %get-tuple-element.286, ...), kind=kLoop, calls=%fused_computation.9.clone.1 | loop fusion | flops 35387520 | bytes 2056704 | tf_op jit(solution)/shard_map/while/body/eval_jaxpr/reduce_sum | solution.py:49
  97.6 4.2 %select_add_fusion.5 = f32[4,384,384]{2,1,0:T(8,128)} fusion(f32[4,384,384]{2,1,0:T(8,128)} %get-tuple-element.315, bf16[5,512,384]{2,1,0:T(8,128)(2,1)S(1)} %get-tuple-element.296, pred[]{:T(512)S(6)} %compare.3), kind=kOutput, calls=%fused_computation.18.clone.1 | convolution fusion | flops 605159424 | bytes 8257537 | tf_op jit(solution)/shard_map/while/body/eval_jaxpr/ltx,lty->lxy/dot_general | solution.py:50
  104.3 4.0 %convert_reduce_fusion.2 = (f32[5,384]{1,0:T(8,128)S(1)}, bf16[5,512,384]{2,1,0:T(8,128)(2,1)S(1)}) fusion(bf16[512]{0:T(512)(128)(2,1)S(1)} %fusion.31, s32[5,512]{1,0:T(8,128)S(1)} %get-tuple-element.281, s32[5,512]{1,0:T(8,128)S(1)} %get-tuple-element.282, s32[5,512]{1,0:T(8,128)S(1)} %get-tuple-element.285, s32[5,512]{1,0:T(8,128)S(1)} %get-tuple-element.286, ...), kind=kLoop, calls=%fused_computation.9.clone.1 | loop fusion | flops 35387520 | bytes 2056704 | tf_op jit(solution)/shard_map/while/body/eval_jaxpr/reduce_sum | solution.py:49
  108.4 4.2 %select_add_fusion.5 = f32[4,384,384]{2,1,0:T(8,128)} fusion(f32[4,384,384]{2,1,0:T(8,128)} %get-tuple-element.315, bf16[5,512,384]{2,1,0:T(8,128)(2,1)S(1)} %get-tuple-element.296, pred[]{:T(512)S(6)} %compare.3), kind=kOutput, calls=%fused_computation.18.clone.1 | convolution fusion | flops 605159424 | bytes 8257537 | tf_op jit(solution)/shard_map/while/body/eval_jaxpr/ltx,lty->lxy/dot_general | solution.py:50
  119.1 4.2 %select_add_fusion.5 = f32[4,384,384]{2,1,0:T(8,128)} fusion(f32[4,384,384]{2,1,0:T(8,128)} %get-tuple-element.315, bf16[5,512,384]{2,1,0:T(8,128)(2,1)S(1)} %get-tuple-element.296, pred[]{:T(512)S(6)} %compare.3), kind=kOutput, calls=%fused_computation.18.clone.1 | convolution fusion | flops 605159424 | bytes 8257537 | tf_op jit(solution)/shard_map/while/body/eval_jaxpr/ltx,lty->lxy/dot_general | solution.py:50
  130.1 4.2 %select_add_fusion.5 = f32[4,384,384]{2,1,0:T(8,128)} fusion(f32[4,384,384]{2,1,0:T(8,128)} %get-tuple-element.315, bf16[5,512,384]{2,1,0:T(8,128)(2,1)S(1)} %get-tuple-element.296, pred[]{:T(512)S(6)} %compare.3), kind=kOutput, calls=%fused_computation.18.clone.1 | convolution fusion | flops 605159424 | bytes 8257537 | tf_op jit(solution)/shard_map/while/body/eval_jaxpr/ltx,lty->lxy/dot_general | solution.py:50
  140.9 4.2 %select_add_fusion.5 = f32[4,384,384]{2,1,0:T(8,128)} fusion(f32[4,384,384]{2,1,0:T(8,128)} %get-tuple-element.315, bf16[5,512,384]{2,1,0:T(8,128)(2,1)S(1)} %get-tuple-element.296, pred[]{:T(512)S(6)} %compare.3), kind=kOutput, calls=%fused_computation.18.clone.1 | convolution fusion | flops 605159424 | bytes 8257537 | tf_op jit(solution)/shard_map/while/body/eval_jaxpr/ltx,lty->lxy/dot_general | solution.py:50
  151.6 4.2 %select_add_fusion.5 = f32[4,384,384]{2,1,0:T(8,128)} fusion(f32[4,384,384]{2,1,0:T(8,128)} %get-tuple-element.315, bf16[5,512,384]{2,1,0:T(8,128)(2,1)S(1)} %get-tuple-element.296, pred[]{:T(512)S(6)} %compare.3), kind=kOutput, calls=%fused_computation.18.clone.1 | convolution fusion | flops 605159424 | bytes 8257537 | tf_op jit(solution)/shard_map/while/body/eval_jaxpr/ltx,lty->lxy/dot_general | solution.py:50
  162.3 4.2 %select_add_fusion.5 = f32[4,384,384]{2,1,0:T(8,128)} fusion(f32[4,384,384]{2,1,0:T(8,128)} %get-tuple-element.315, bf16[5,512,384]{2,1,0:T(8,128)(2,1)S(1)} %get-tuple-element.296, pred[]{:T(512)S(6)} %compare.3), kind=kOutput, calls=%fused_computation.18.clone.1 | convolution fusion | flops 605159424 | bytes 8257537 | tf_op jit(solution)/shard_map/while/body/eval_jaxpr/ltx,lty->lxy/dot_general | solution.py:50
  173.1 4.2 %select_add_fusion.5 = f32[4,384,384]{2,1,0:T(8,128)} fusion(f32[4,384,384]{2,1,0:T(8,128)} %get-tuple-element.315, bf16[5,512,384]{2,1,0:T(8,128)(2,1)S(1)} %get-tuple-element.296, pred[]{:T(512)S(6)} %compare.3), kind=kOutput, calls=%fused_computation.18.clone.1 | convolution fusion | flops 605159424 | bytes 8257537 | tf_op jit(solution)/shard_map/while/body/eval_jaxpr/ltx,lty->lxy/dot_general | solution.py:50
  177.4 34.7 %reduce-scatter.3.cloned.1.call-done = f32[4,96,384]{2,1,0:T(8,128)} async-done(((f32[4,384,384]{2,1,0:T(8,128)}), f32[4,96,384]{2,1,0:T(8,128)}) %reduce-scatter.3.cloned.1.call-update) | async-done | bytes 589840 | tf_op jit(solution)/shard_map/reduce_scatter | solution.py:22
  212.1 21.3 %reduce-scatter.5.cloned.1.call-done = f32[4,48,384]{2,1,0:T(8,128)} async-done(((f32[4,96,384]{2,1,0:T(8,128)}), f32[4,48,384]{2,1,0:T(8,128)}) %reduce-scatter.5.cloned.1.call-update) | async-done | bytes 294928 | tf_op jit(solution)/shard_map/reduce_scatter | solution.py:22
  234.1 17.4 %all-reduce.1 = (f32[5,384]{1,0:T(8,128)S(1)}, f32[]{:T(128)}) all-reduce(f32[5,384]{1,0:T(8,128)S(1)} %get-tuple-element.137, f32[]{:T(128)S(6)} %convert_element_type.78), channel_id=1, replica_groups=mesh['tok_0'=4,'tok_1'=2,'tok_2'=2,'own_0'=4,'own_1'=2] {'tok_0'}, use_global_device_ids=true, to_apply=%region_11.0 | all-reduce | flops 1921 | bytes 15368 | tf_op jit(solution)/shard_map/psum | solution.py:16
  251.5 8.5 %all-reduce.4 = (f32[5,384]{1,0:T(8,128)S(1)}, f32[]{:T(128)}) all-reduce(f32[5,384]{1,0:T(8,128)S(1)} %get-tuple-element.202, f32[]{:T(128)} %get-tuple-element.203), channel_id=1, replica_groups=mesh['tok_0'=4,'tok_1'=2,'tok_2'=2,'own_0'=4,'own_1'=2] {'tok_1'}, use_global_device_ids=true, to_apply=%region_12.0 | all-reduce | flops 1921 | bytes 15368 | tf_op jit(solution)/shard_map/psum | solution.py:16
  260.0 4.4 %all-reduce.3 = (f32[5,384]{1,0:T(8,128)S(1)}, f32[]{:T(128)}) all-reduce(f32[5,384]{1,0:T(8,128)S(1)} %get-tuple-element.208, f32[]{:T(128)} %get-tuple-element.209), channel_id=1, replica_groups=mesh['tok_0'=4,'tok_1'=2,'tok_2'=2,'own_0'=4,'own_1'=2] {'tok_2'}, use_global_device_ids=true, to_apply=%region_13.0 | all-reduce | flops 1921 | bytes 15368 | tf_op jit(solution)/shard_map/psum | solution.py:16
  264.4 18.2 %all-reduce = (f32[5,384]{1,0:T(8,128)S(1)}, f32[]{:T(128)}) all-reduce(f32[5,384]{1,0:T(8,128)S(1)} %get-tuple-element.206, f32[]{:T(128)} %get-tuple-element.207), channel_id=1, replica_groups=mesh['tok_0'=4,'tok_1'=2,'tok_2'=2,'own_0'=4,'own_1'=2] {'own_0'}, use_global_device_ids=true, to_apply=%region_14.0 | all-reduce | flops 1921 | bytes 15368 | tf_op jit(solution)/shard_map/psum | solution.py:16
  282.6 11.1 %all-reduce.2 = (f32[5,384]{1,0:T(8,128)S(1)}, f32[]{:T(128)}) all-reduce(f32[5,384]{1,0:T(8,128)S(1)} %get-tuple-element.200, f32[]{:T(128)} %get-tuple-element.201), channel_id=1, replica_groups=mesh['tok_0'=4,'tok_1'=2,'tok_2'=2,'own_0'=4,'own_1'=2] {'own_1'}, use_global_device_ids=true, to_apply=%region_15.0 | all-reduce | flops 1921 | bytes 15368 | tf_op jit(solution)/shard_map/psum | solution.py:16
  (133 shorter events, 74.3 us)
Async XLA Ops:
  6.5 205.5 %reduce-scatter.3.cloned.1.call-start = ((), (), s32[]{:S(2)}) async-start(), calls=%async_computation.2 | async-start | bytes 2949120 | tf_op jit(solution)/shard_map/reduce_scatter | solution.py:22
  177.3 56.1 %reduce-scatter.5.cloned.1.call-start = ((), (), s32[]{:S(2)}) async-start(), calls=%async_computation.3 | async-start | bytes 884736 | tf_op jit(solution)/shard_map/reduce_scatter | solution.py:22
  212.1 81.7 %all-gather.3.cloned.1.call-start = ((), (), s32[]{:S(2)}) async-start(), calls=%async_computation.4 | async-start | bytes 5013504 | tf_op jit(solution)/shard_map/all_gather | solution.py:27
Sparse Core Ops, SparseCore 0:
  177.5 34.5 reduce-scatter.2
  214.4 18.9 reduce-scatter.4
  235.2 37.4 all-gather.2
where the time goes:
time: 306 us; the launch traced here: 304 us
  other arithmetic  78.8 us (26%)
  matrix products  66 us (22%)
  blocking collectives  59.6 us (19%)
  waiting for transfers between devices  56 us (18%)
  local copies, waits for them, and re-layouts  29 us (9%)
  between operations  13.8 us (5%)
    dot_general x16, matrix products, one_block(): jnp.einsum('ltx,lty->lxy', hot[:-1], hot[1:], preferred_element_type=jnp....  66 us
    reduce_sum x16, other arithmetic, one_block(): counts = counts + jnp.sum(hot, axis=1, dtype=jnp.float32)  64.3 us
    psum x5, blocking collectives, over_axes(): return functools.reduce(lax.psum, axes, shard)  59.6 us
    reduce_scatter x2, waiting for transfers between devices, sum_by_axis(): nearer = lax.psum_scatter(shard, axes[0], scatter_dimension=dim, tiled=True)  56 us
    slice x16, local copies, waits for them, and re-layouts, one_block(): hot = hot + (piece[:, slot, :, None] == columns).astype(jnp.bfloat16)  28.5 us
    convert_element_type x16, other arithmetic, one_block(): alive = (rows < limit).astype(jnp.bfloat16)  10.4 us
  transfers between devices with their start and end apart: 3, of which 2 were waited for; matrix products, arithmetic and copies ran while one was open for 0% of the time, Pallas kernels for 0%

commit v1 on v0

v1 whole, which is shorter than its diff:
```python
import functools

import jax
import jax.numpy as jnp
import numpy as np
from jax import lax
from jax.experimental import pallas as pl
from jax.experimental.pallas import tpu as pltpu
from jax.sharding import Mesh
from jax.sharding import PartitionSpec as P

E = 384
HOT = jnp.float8_e4m3fn
DEAD = 511
BLOCK = 2048
PIECE = 512
TILES = 40
COUNT_TILE = 36

ALL = ("tok", "own")
AXES = {"x": 4, "yl": 2, "c": 2, "z": 4, "yh": 2}


def groups(axes):
    names = list(AXES)
    rest = [a for a in names if a not in axes]
    order = [names.index(a) for a in rest + list(axes)]
    index = np.arange(128).reshape(tuple(AXES.values()))
    size = int(np.prod([AXES[a] for a in axes]))
    return index.transpose(order).reshape(-1, size).tolist()


def fill_hot(ids, hot, row0):
    tokens = ids.shape[1]
    low = ids & 15
    bit = jnp.left_shift(1, lax.shift_right_logical(ids, 4))
    word = lax.broadcasted_iota(jnp.int32, (16, tokens), 0)
    mask = jnp.zeros((16, tokens), jnp.int32)
    for k in range(ids.shape[0]):
        mask = mask | jnp.where(word == low[k : k + 1], bit[k : k + 1], 0)
    for half in range(2):
        part = (lax.shift_right_logical(mask, 12 * half) & 0xFFF).astype(jnp.int16)
        for b in range(12):
            one = jnp.where((part & jnp.int16(1 << b)) != 0, jnp.bfloat16(1), jnp.bfloat16(0))
            row = row0 + half * 192 + b * 16
            hot[row : row + 16, :] = one.astype(HOT)


def count_pairs(limit, layers, acc, hots, slots):
    steps = slots // BLOCK

    def fill(i, hot):
        for layer, read in enumerate(layers):
            for s in range(0, BLOCK, PIECE):
                start = pl.multiple_of(i * BLOCK + s, PIECE)
                ids = read(start)
                if limit is not None:
                    pos = start + lax.broadcasted_iota(jnp.int32, ids.shape, 1)
                    ids = jnp.where(pos < limit, ids, DEAD)
                fill_hot(ids, hot.at[:, s : s + PIECE], layer * E)

    def multiply(hot):
        acc[...] += lax.dot_general(
            hot[2 * E :, :], hot[: 2 * E, :], (((1,), (1,)), ((), ())), preferred_element_type=jnp.float32
        )

    fill(0, hots[0])

    @pl.loop(0, steps // 2)
    def _(i):
        fill(2 * i + 1, hots[1])
        multiply(hots[0])

        @pl.when(2 * i + 2 < steps)
        def _():
            fill(2 * i + 2, hots[0])

        multiply(hots[1])


def own_kernel(core_ref, limit_ref, a_ref, b_ref, c_ref, acc, hot0, hot1):
    acc[...] = jnp.zeros_like(acc)
    layers = [lambda s, r=r: r[0, :, pl.ds(s, PIECE)] for r in (a_ref, c_ref, b_ref)]
    count_pairs(limit_ref[0], layers, acc, (hot0, hot1), a_ref.shape[2])


def peer_kernel(ids_ref, start_ref, out_ref, acc, hot0, hot1):
    acc[...] = start_ref[...]
    layers = [lambda s, l=l: ids_ref[l, :, pl.ds(s, PIECE)] for l in (0, 2, 1)]
    count_pairs(None, layers, acc, (hot0, hot1), ids_ref.shape[2])
    first = jnp.transpose(acc[:, :E])
    acc[:, :E] = first
    for owner in range(8):
        for pair in range(2):
            for r in range(6):
                for c in range(3):
                    row = 48 * owner + 8 * r
                    col = E * pair + 128 * c
                    out_ref[owner, (pair * 6 + r) * 3 + c] = acc[row : row + 8, col : col + 128]
    count = jnp.sum(acc[...], axis=0, keepdims=True) * 0.125
    rows = [count[:, 128 * i : 128 * i + 128] for i in range(6)] + [jnp.zeros((2, 128), jnp.float32)]
    tile = jnp.concatenate(rows, axis=0)
    for owner in range(8):
        out_ref[owner, COUNT_TILE] = tile
        out_ref[owner, COUNT_TILE + 1 :] = jnp.zeros((TILES - COUNT_TILE - 1, 8, 128), jnp.float32)


def lift_kernel(core_ref, mine_ref, other_ref, out_ref):
    core = core_ref[0]
    for half, ref in ((core, mine_ref), (1 - core, other_ref)):
        counts = ref[COUNT_TILE]
        total = jnp.sum(counts[0:3, :]) * 0.125
        for pair in range(2):
            for r in range(6):
                base = (pair * 6 + r) * 3
                tiles = [ref[base + c] for c in range(3)]
                left = jnp.sum(tiles[0] + tiles[1] + tiles[2], axis=1, keepdims=True) * 0.125
                for c in range(3):
                    right = counts[3 * pair + c : 3 * pair + c + 1, :]
                    value = tiles[c] * total / jnp.maximum(left * right, 1.0)
                    out_ref[2 * half + pair, 8 * r : 8 * r + 8, 128 * c : 128 * c + 128] = value


def shards(expert_ids, shard_length):
    slots = expert_ids.shape[2]
    core = lax.axis_index("tok") & 1
    core_arg = core.reshape(1).astype(jnp.int32)
    live = lax.broadcasted_iota(jnp.int32, (1, 1, slots), 2) < shard_length[0]
    send = lax.dynamic_slice_in_dim(expert_ids, 2 * (1 - core), 3, 0)
    send = jnp.where(live, send, DEAD)
    peer = lax.ppermute(send, ALL, [(i, i ^ 8) for i in range(128)])

    params = pltpu.CompilerParams(vmem_limit_bytes=32 * 1024 * 1024)
    flops = 2 * slots * E * 2 * E
    hots = [pltpu.VMEM((3 * E, BLOCK), HOT)] * 2
    layer = lambda k: pl.BlockSpec((1, 8, slots), lambda i, c: (2 * c[0] + k, 0, 0))
    start = pl.pallas_call(
        own_kernel,
        grid_spec=pltpu.PrefetchScalarGridSpec(
            num_scalar_prefetch=1,
            grid=(1,),
            in_specs=[pl.BlockSpec(memory_space=pltpu.SMEM), layer(0), layer(1), layer(2)],
            out_specs=pl.BlockSpec((E, 2 * E), lambda i, c: (0, 0)),
            scratch_shapes=hots,
        ),
        out_shape=jax.ShapeDtypeStruct((E, 2 * E), jnp.float32),
        compiler_params=params,
        cost_estimate=pl.CostEstimate(flops=flops, bytes_accessed=2 << 20, transcendentals=0),
        name="own_tokens",
    )(core_arg, shard_length, expert_ids, expert_ids, expert_ids)
    chunk = pl.pallas_call(
        peer_kernel,
        out_shape=jax.ShapeDtypeStruct((8, TILES, 8, 128), jnp.float32),
        scratch_shapes=[pltpu.VMEM((E, 2 * E), jnp.float32)] + hots,
        compiler_params=params,
        cost_estimate=pl.CostEstimate(flops=flops, bytes_accessed=2 << 20, transcendentals=0),
        name="peer_tokens",
    )(peer, start)

    parts = chunk.reshape(64, TILES, 128)
    parts = lax.all_to_all(
        parts, ALL, 0, 0, axis_index_groups=groups(["z", "yh", "x", "yl"]), tiled=True
    )
    piece = parts.sum(axis=0)
    spread = jnp.broadcast_to(piece[None], (8, TILES, 128))
    whole = lax.all_to_all(spread, ALL, 0, 0, axis_index_groups=groups(["x", "yl"]), tiled=True)
    mine = whole.reshape(TILES, 8, 128)
    other = lax.ppermute(mine, ALL, [(i, i ^ 8) for i in range(128)])
    return pl.pallas_call(
        lift_kernel,
        in_specs=[pl.BlockSpec(memory_space=pltpu.SMEM)] + [pl.BlockSpec(memory_space=pltpu.VMEM)] * 2,
        out_shape=jax.ShapeDtypeStruct((4, E // 8, E), jnp.float32),
        name="lift",
    )(core_arg, mine, other)


def solution(mesh):
    torus = Mesh(mesh.devices.reshape(16, 8), ALL)
    return jax.shard_map(
        shards,
        mesh=torus,
        in_specs=(P(None, None, ALL), P(ALL)),
        out_specs=P(None, "own", None),
        check_vma=False,
    )
```

time: 306 us -> 65.5 us (0.21)
  the two profiles are of different devices: /device:TPU:0 before, /device:TPU:1 now
where the time goes in v1:
time: 65.5 us; the launch traced here: 65.2 us
  blocking collectives  39.9 us (61%)
  Pallas kernels  17.4 us (27%)
  starting transfers between devices  4.06 us (6%)
  other arithmetic  1.33 us (2%)
  waiting for transfers between devices  1.03 us (2%)
  between operations  0.8 us (1%)
  local copies, waits for them, and re-layouts  0.69 us (1%)
    all_to_all x1, blocking collectives, shards(): lax.all_to_all(parts, ALL, 0, 0, axis_index_groups=groups(['z', 'yh', 'x'...  32.1 us
    pallas_call x1, Pallas kernels, shards(): pl.pallas_call(peer_kernel, out_shape=jax.ShapeDtypeStruct((8, TILES, 8,...  7.85 us
    all_to_all x1, blocking collectives, shards(): lax.all_to_all(spread, ALL, 0, 0, axis_index_groups=groups(['x', 'yl']),...  7.79 us
    pallas_call x1, Pallas kernels, shards(): pl.pallas_call(own_kernel, grid_spec=pltpu.PrefetchScalarGridSpec(num_sca...  7.72 us
    ppermute x1, starting transfers between devices, shards(): other = lax.ppermute(mine, ALL, [(i, i ^ 8) for i in range(128)])  2.6 us
    pallas_call x1, Pallas kernels, shards(): pl.pallas_call(lift_kernel, in_specs=[pl.BlockSpec(memory_space=pltpu.SME...  1.86 us
    ppermute x1, starting transfers between devices, shards(): peer = lax.ppermute(send, ALL, [(i, i ^ 8) for i in range(128)])  1.46 us
  transfers between devices with their start and end apart: 2, of which 1 were waited for; matrix products, arithmetic and copies ran while one was open for 0% of the time, Pallas kernels for 12%

profile of v1, /device:TPU:1, one launch (start us, length us, event | category | flops | bytes accessed | tf_op | source)
XLA Modules:
  0.0 65.2 jit_solution(7702290192657934279)
XLA Ops:
  0.0 0.0 copy-start
  0.8 1.2 %dynamic-slice_select_fusion = s32[3,8,8192]{2,1,0:T(8,128)S(1)} fusion(s32[5,8,8192]{2,1,0:T(8,128)} %c_ref.1, s32[]{:T(128)S(6)} %select_n.7, pred[8192]{0:T(1024)(128)(4,1)S(1)} %iota_compare_fusion), kind=kLoop, calls=%fused_computation | loop fusion | flops 196608 | bytes 1581060 | tf_op jit(solution)/shard_map/jit(_where)/select_n | solution.py:130
  2.0 1.5 %collective-permute-start = (s32[3,8,8192]{2,1,0:T(8,128)S(1)}, s32[3,8,8192]{2,1,0:T(8,128)S(1)}, u32[]{:S(2)}, u32[]{:S(2)}) collective-permute-start(s32[3,8,8192]{2,1,0:T(8,128)S(1)} %dynamic-slice_select_fusion), channel_id=1, source_target_pairs={{0,8},{1,9},{2,10},{3,11},{4,12},{5,13},{6,14},{7,15},{8,0},{9,1},... | collective-permute-start | bytes 2359304 | tf_op jit(solution)/shard_map/ppermute | solution.py:131
  3.5 0.0 copy-done
  3.5 7.7 %own_tokens.1.start_ref = f32[384,768]{1,0:T(8,128)S(1)} custom-call(s32[1]{0:T(128)} %bitcast.core_ref, s32[1]{0:T(128)} %copy.3.limit_ref, s32[5,8,8192]{2,1,0:T(8,128)S(1)} %copy-done, s32[5,8,8192]{2,1,0:T(8,128)S(1)} %copy-done, s32[5,8,8192]{2,1,0:T(8,128)S(1)} %copy-done), custom_call_target="tpu_custom_call" | custom-call | flops 4831838208 | bytes 2097152 | tf_op jit(solution)/shard_map/own_tokens/pallas_call | solution.py:137
  11.2 0.0 collective-permute-done.ids_ref
  11.2 7.9 %peer_tokens.1 = f32[8,40,8,128]{3,2,1,0:T(8,128)S(1)} custom-call(s32[3,8,8192]{2,1,0:T(8,128)S(1)} %collective-permute-done.ids_ref, f32[384,768]{1,0:T(8,128)S(1)} %own_tokens.1.start_ref), custom_call_target="tpu_custom_call" | custom-call | flops 4831838208 | bytes 2097152 | tf_op jit(solution)/shard_map/peer_tokens/pallas_call | solution.py:151
  19.0 32.1 %all_to_all.10 = f32[64,40,128]{2,1,0:T(8,128)S(1)} all-to-all(f32[64,40,128]{2,1,0:T(8,128)S(1)} %bitcast.5), channel_id=1, replica_groups={{0,16,32,48,64,80,96,112,1,17,33,49,65,81,97,113,2,18,34,50,66,82,98,11..., dimensions={0} | all-to-all | bytes 2621440 | tf_op jit(solution)/shard_map/all_to_all | solution.py:161
  51.2 0.1 reduce_sum.9
  51.3 7.8 %all_to_all.11 = f32[8,40,128]{2,1,0:T(8,128)S(1)} all-to-all(f32[8,40,128]{2,1,0:T(8,128)S(1)} %broadcast_in_dim.20), channel_id=1, replica_groups={{0,16,32,48,64,80,96,112},{1,17,33,49,65,81,97,113},{2,18,34,50,66,82,9..., dimensions={0} | all-to-all | bytes 327680 | tf_op jit(solution)/shard_map/all_to_all | solution.py:166
  59.1 0.0 copy-start.1
  59.1 2.6 %collective-permute-start.1 = (f32[40,8,128]{2,1,0:T(8,128)S(1)}, f32[40,8,128]{2,1,0:T(8,128)S(1)}, u32[]{:S(2)}, u32[]{:S(2)}) collective-permute-start(f32[40,8,128]{2,1,0:T(8,128)S(1)} %bitcast.6), channel_id=1, source_target_pairs={{0,8},{1,9},{2,10},{3,11},{4,12},{5,13},{6,14},{7,15},{8,0},{9,1},... | collective-permute-start | bytes 491528 | tf_op jit(solution)/shard_map/ppermute | solution.py:168
  61.7 1.0 %collective-permute-done.1.other_ref = f32[40,8,128]{2,1,0:T(8,128)S(1)} collective-permute-done((f32[40,8,128]{2,1,0:T(8,128)S(1)}, f32[40,8,128]{2,1,0:T(8,128)S(1)}, u32[]{:S(2)}, u32[]{:S(2)}) %collective-permute-start.1) | collective-permute-done | bytes 163872 | tf_op jit(solution)/shard_map/ppermute | solution.py:168
  62.7 0.0 copy-done.1
  62.7 0.0 copy-start.2
  62.7 0.7 %copy-done.2 = f32[40,8,128]{2,1,0:T(8,128)} copy-done((f32[40,8,128]{2,1,0:T(8,128)}, f32[40,8,128]{2,1,0:T(8,128)S(1)}, u32[]{:S(2)}) %copy-start.2) | copy-done | bytes 163864
  63.4 1.9 %lift.1 = f32[4,48,384]{2,1,0:T(8,128)} custom-call(s32[1]{0:T(128)} %bitcast.core_ref, f32[40,8,128]{2,1,0:T(8,128)} %bitcast.7, f32[40,8,128]{2,1,0:T(8,128)} %copy-done.2), custom_call_target="tpu_custom_call" | custom-call | tf_op jit(solution)/shard_map/lift/pallas_call | solution.py:169
  (2 shorter events, 0.0 us)
Async XLA Ops:
  0.0 3.5 %copy-start = (s32[5,8,8192]{2,1,0:T(8,128)S(1)}, s32[5,8,8192]{2,1,0:T(8,128)}, u32[]{:S(2)}) copy-start(s32[5,8,8192]{2,1,0:T(8,128)} %c_ref.1) | copy-start | bytes 3932164
  2.0 9.2 %collective-permute-start = (s32[3,8,8192]{2,1,0:T(8,128)S(1)}, s32[3,8,8192]{2,1,0:T(8,128)S(1)}, u32[]{:S(2)}, u32[]{:S(2)}) collective-permute-start(s32[3,8,8192]{2,1,0:T(8,128)S(1)} %dynamic-slice_select_fusion), channel_id=1, source_target_pairs={{0,8},{1,9},{2,10},{3,11},{4,12},{5,13},{6,14},{7,15},{8,0},{9,1},... | collective-permute-start | bytes 2359304 | tf_op jit(solution)/shard_map/ppermute | solution.py:131
  59.1 3.6 %copy-start.1 = (f32[8,40,128]{2,1,0:T(8,128)}, f32[8,40,128]{2,1,0:T(8,128)S(1)}, u32[]{:S(2)}) copy-start(f32[8,40,128]{2,1,0:T(8,128)S(1)} %all_to_all.11) | copy-start | bytes 491524
  59.1 3.6 %collective-permute-start.1 = (f32[40,8,128]{2,1,0:T(8,128)S(1)}, f32[40,8,128]{2,1,0:T(8,128)S(1)}, u32[]{:S(2)}, u32[]{:S(2)}) collective-permute-start(f32[40,8,128]{2,1,0:T(8,128)S(1)} %bitcast.6), channel_id=1, source_target_pairs={{0,8},{1,9},{2,10},{3,11},{4,12},{5,13},{6,14},{7,15},{8,0},{9,1},... | collective-permute-start | bytes 491528 | tf_op jit(solution)/shard_map/ppermute | solution.py:168
  62.7 0.7 %copy-start.2 = (f32[40,8,128]{2,1,0:T(8,128)}, f32[40,8,128]{2,1,0:T(8,128)S(1)}, u32[]{:S(2)}) copy-start(f32[40,8,128]{2,1,0:T(8,128)S(1)} %collective-permute-done.1.other_ref) | copy-start | bytes 491524

commit v2 on v1

v2 whole, which is shorter than its diff:
```python
import functools

import jax
import jax.numpy as jnp
import numpy as np
from jax import lax
from jax.experimental import pallas as pl
from jax.experimental.pallas import tpu as pltpu
from jax.sharding import Mesh
from jax.sharding import PartitionSpec as P

E = 384
HOT = jnp.float8_e4m3fn
DEAD = 511
BLOCK = 2048
PIECE = 512
TILES = 40
COUNT_TILE = 36

ALL = ("tok", "own")
AXES = {"x": 4, "yl": 2, "c": 2, "z": 4, "yh": 2}


def groups(axes):
    names = list(AXES)
    rest = [a for a in names if a not in axes]
    order = [names.index(a) for a in rest + list(axes)]
    index = np.arange(128).reshape(tuple(AXES.values()))
    size = int(np.prod([AXES[a] for a in axes]))
    return index.transpose(order).reshape(-1, size).tolist()


def fill_hot(ids, hot, row0):
    tokens = ids.shape[1]
    low = ids & 15
    bit = jnp.left_shift(1, lax.shift_right_logical(ids, 4))
    word = lax.broadcasted_iota(jnp.int32, (16, tokens), 0)
    mask = jnp.zeros((16, tokens), jnp.int32)
    one, zero = jnp.bfloat16(1), jnp.bfloat16(0)
    for k in range(ids.shape[0]):
        mask = mask | jnp.where(word == low[k : k + 1], bit[k : k + 1], 0)
    for half in range(2):
        part = (lax.shift_right_logical(mask, 12 * half) & 0xFFF).astype(jnp.int16)
        for b in range(0, 12, 2):
            ones = [jnp.where((part & jnp.int16(1 << n)) != 0, one, zero) for n in (b, b + 1)]
            row = row0 + half * 192 + b * 16
            hot[row : row + 32, :] = jnp.concatenate(ones, axis=0).astype(HOT)


def add_pairs(core, limit, ids_ref, acc, hot):
    @pl.loop(0, ids_ref.shape[2] // BLOCK)
    def _(i):
        for place, layer in enumerate((0, 2, 1)):
            for s in range(0, BLOCK, PIECE):
                start = pl.multiple_of(i * BLOCK + s, PIECE)
                ids = ids_ref[2 * core + layer, :, pl.ds(start, PIECE)]
                slot = start + lax.broadcasted_iota(jnp.int32, ids.shape, 1)
                ids = jnp.where(slot < limit, ids, DEAD)
                fill_hot(ids, hot.at[:, s : s + PIECE], place * E)
        acc[...] += lax.dot_general(
            hot[2 * E :, :], hot[: 2 * E, :], (((1,), (1,)), ((), ())), preferred_element_type=jnp.float32
        )


def own_kernel(core_ref, limit_ref, ids_ref, acc, hot):
    acc[...] = jnp.zeros_like(acc)
    add_pairs(core_ref[0], limit_ref[0], ids_ref, acc, hot)


def peer_kernel(core_ref, limit_ref, ids_ref, start_ref, out_ref, acc, hot):
    acc[...] = start_ref[...]
    add_pairs(core_ref[0], limit_ref[0], ids_ref, acc, hot)
    count = jnp.sum(acc[...], axis=0, keepdims=True) * 0.125
    acc[:, :E] = jnp.transpose(acc[:, :E])
    for owner in range(8):
        for pair in range(2):
            for r in range(6):
                for c in range(3):
                    row = 48 * owner + 8 * r
                    col = E * pair + 128 * c
                    out_ref[owner, (pair * 6 + r) * 3 + c] = acc[row : row + 8, col : col + 128]
    count_b = jnp.sum(acc[:, :E], axis=0, keepdims=True) * 0.125
    rows = [count_b[:, 128 * i : 128 * i + 128] for i in range(3)]
    rows += [count[:, E + 128 * i : E + 128 * i + 128] for i in range(3)]
    tile = jnp.concatenate(rows + [jnp.zeros((2, 128), jnp.float32)], axis=0)
    for owner in range(8):
        out_ref[owner, COUNT_TILE] = tile
        out_ref[owner, COUNT_TILE + 1 :] = jnp.zeros((TILES - COUNT_TILE - 1, 8, 128), jnp.float32)


def lift_kernel(core_ref, mine_ref, other_ref, out_ref):
    core = core_ref[0]
    for half, ref in ((core, mine_ref), (1 - core, other_ref)):
        counts = ref[COUNT_TILE]
        total = jnp.sum(counts[0:3, :]) * 0.125
        for pair in range(2):
            for r in range(6):
                base = (pair * 6 + r) * 3
                tiles = [ref[base + c] for c in range(3)]
                left = jnp.sum(tiles[0] + tiles[1] + tiles[2], axis=1, keepdims=True) * 0.125
                for c in range(3):
                    right = counts[3 * pair + c : 3 * pair + c + 1, :]
                    value = tiles[c] * total / jnp.maximum(left * right, 1.0)
                    out_ref[2 * half + pair, 8 * r : 8 * r + 8, 128 * c : 128 * c + 128] = value


def shards(expert_ids, shard_length):
    slots = expert_ids.shape[2]
    core = (lax.axis_index("tok") & 1).reshape(1).astype(jnp.int32)
    swap = [(i, i ^ 8) for i in range(128)]
    peer_ids = lax.ppermute(expert_ids, ALL, swap)
    peer_limit = lax.ppermute(shard_length, ALL, swap)

    params = pltpu.CompilerParams(vmem_limit_bytes=24 * 1024 * 1024)
    flops = 2 * slots * E * 2 * E
    smem = pl.BlockSpec(memory_space=pltpu.SMEM)
    vmem = pl.BlockSpec(memory_space=pltpu.VMEM)
    hot = pltpu.VMEM((3 * E, BLOCK), HOT)
    start = pl.pallas_call(
        own_kernel,
        in_specs=[smem, smem, vmem],
        out_specs=vmem,
        out_shape=jax.ShapeDtypeStruct((E, 2 * E), jnp.float32),
        scratch_shapes=[hot],
        compiler_params=params,
        cost_estimate=pl.CostEstimate(flops=flops, bytes_accessed=2 << 20, transcendentals=0),
        name="own_tokens",
    )(core, shard_length, expert_ids)
    chunk = pl.pallas_call(
        peer_kernel,
        in_specs=[smem, smem, vmem, vmem],
        out_specs=vmem,
        out_shape=jax.ShapeDtypeStruct((8, TILES, 8, 128), jnp.float32),
        scratch_shapes=[pltpu.VMEM((E, 2 * E), jnp.float32), hot],
        compiler_params=params,
        cost_estimate=pl.CostEstimate(flops=flops, bytes_accessed=2 << 20, transcendentals=0),
        name="peer_tokens",
    )(core, peer_limit, peer_ids, start)

    half = TILES // 2
    parts = lax.all_to_all(
        chunk.reshape(16, 8 * half, 128), ALL, 0, 0, axis_index_groups=groups(["z", "yh", "yl"]), tiled=True
    )
    piece = parts.sum(axis=0)
    spread = jnp.broadcast_to(piece[None], (8, 8 * half, 128))
    whole = lax.all_to_all(spread, ALL, 0, 0, axis_index_groups=groups(["x", "yl"]), tiled=True)
    mine = whole.reshape(4, TILES, 8, 128).sum(axis=0)
    other = lax.ppermute(mine, ALL, swap)
    return pl.pallas_call(
        lift_kernel,
        in_specs=[smem, vmem, vmem],
        out_specs=vmem,
        out_shape=jax.ShapeDtypeStruct((4, E // 8, E), jnp.float32),
        compiler_params=pltpu.CompilerParams(vmem_limit_bytes=8 * 1024 * 1024),
        name="lift",
    )(core, mine, other)


def solution(mesh):
    torus = Mesh(mesh.devices.reshape(16, 8), ALL)
    return jax.shard_map(
        shards,
        mesh=torus,
        in_specs=(P(None, None, ALL), P(ALL)),
        out_specs=P(None, "own", None),
        check_vma=False,
    )
```

time: 65.5 us -> 60 us (0.916)
  Pallas kernels: 17.4 us -> 12 us
  other arithmetic: 1.33 us -> 0.1 us
  local copies, waits for them, and re-layouts: 0.69 us -> 1.35 us
    pallas_call x3, Pallas kernels: 17.4 us -> 12 us  [the longest x1 5.96 us: shards(): pl.pallas_call(peer_kernel, in_specs=[smem, smem, vmem, vmem], out_specs=...]
    all_to_all x1, blocking collectives: 7.79 us -> 13 us  [shards(): lax.all_to_all(spread, ALL, 0, 0, axis_index_groups=groups(['x', 'yl']),...]
    all_to_all x1, blocking collectives: 32.1 us -> 27 us  [shards(): lax.all_to_all(chunk.reshape(16, 8 * half, 128), ALL, 0, 0, axis_index_gr...]
    select_n x1 -> x0, other arithmetic: 1.21 us -> none  [shards(): send = jnp.where(live, send, DEAD)]
    ppermute x2 -> x3, starting transfers between devices: 4.06 us -> 4.55 us  [the longest x1 3.17 us: shards(): other = lax.ppermute(mine, ALL, swap)]
  transfers between devices with their start and end apart: 2 -> 3, of which waited for: 1 -> 1; matrix products, arithmetic and copies ran while one was open for 0% -> 0% of each run, Pallas kernels for 12% -> 9%
where the time goes in v2:
time: 60 us; the launch traced here: 59.8 us
  blocking collectives  40 us (67%)
  Pallas kernels  12 us (20%)
  starting transfers between devices  4.55 us (8%)
  local copies, waits for them, and re-layouts  1.35 us (2%)
  waiting for transfers between devices  1.03 us (2%)
  between operations  0.71 us (1%)
    all_to_all x1, blocking collectives, shards(): lax.all_to_all(chunk.reshape(16, 8 * half, 128), ALL, 0, 0, axis_index_gr...  27 us
    all_to_all x1, blocking collectives, shards(): lax.all_to_all(spread, ALL, 0, 0, axis_index_groups=groups(['x', 'yl']),...  13 us
    pallas_call x1, Pallas kernels, shards(): pl.pallas_call(peer_kernel, in_specs=[smem, smem, vmem, vmem], out_specs=...  5.96 us
    pallas_call x1, Pallas kernels, shards(): pl.pallas_call(own_kernel, in_specs=[smem, smem, vmem], out_specs=vmem, o...  5.22 us
    ppermute x1, starting transfers between devices, shards(): other = lax.ppermute(mine, ALL, swap)  3.17 us
    ppermute x1, starting transfers between devices, shards(): peer_ids = lax.ppermute(expert_ids, ALL, swap)  1.38 us
    unnamed x2, local copies, waits for them, and re-layouts  1.31 us
  transfers between devices with their start and end apart: 3, of which 1 were waited for; matrix products, arithmetic and copies ran while one was open for 0% of the time, Pallas kernels for 9%

profile of v2, /device:TPU:1, one launch (start us, length us, event | category | flops | bytes accessed | tf_op | source)
XLA Modules:
  0.0 59.8 jit_solution(8323649589713360722)
XLA Ops:
  0.0 1.4 %collective-permute-start.1 = (s32[5,8,8192]{2,1,0:T(8,128)}, s32[5,8,8192]{2,1,0:T(8,128)S(1)}, u32[]{:S(2)}, u32[]{:S(2)}) collective-permute-start(s32[5,8,8192]{2,1,0:T(8,128)} %ids_ref.1), channel_id=1, source_target_pairs={{0,8},{1,9},{2,10},{3,11},{4,12},{5,13},{6,14},{7,15},{8,0},{9,1},... | collective-permute-start | bytes 3932168 | tf_op jit(solution)/shard_map/ppermute | solution.py:111
  1.4 0.0 collective-permute-start
  2.0 0.0 copy-start
  2.0 1.3 %copy-done = s32[5,8,8192]{2,1,0:T(8,128)S(1)} copy-done((s32[5,8,8192]{2,1,0:T(8,128)S(1)}, s32[5,8,8192]{2,1,0:T(8,128)}, u32[]{:S(2)}) %copy-start) | copy-done | bytes 1310744
  3.4 5.2 %own_tokens.1.start_ref = f32[384,768]{1,0:T(8,128)S(1)} custom-call(s32[1]{0:T(128)} %bitcast.core_ref, s32[1]{0:T(128)S(6)} %copy.3.limit_ref, s32[5,8,8192]{2,1,0:T(8,128)S(1)} %copy-done), custom_call_target="tpu_custom_call" | custom-call | flops 4831838208 | bytes 2097152 | tf_op jit(solution)/shard_map/own_tokens/pallas_call | solution.py:119
  8.6 0.0 collective-permute-done.limit_ref
  8.6 0.0 collective-permute-done.1.ids_ref
  8.6 6.0 %peer_tokens.1 = f32[8,40,8,128]{3,2,1,0:T(8,128)S(1)} custom-call(s32[1]{0:T(128)} %bitcast.core_ref, s32[1]{0:T(128)} %collective-permute-done.limit_ref, s32[5,8,8192]{2,1,0:T(8,128)S(1)} %collective-permute-done.1.ids_ref, f32[384,768]{1,0:T(8,128)S(1)} %own_tokens.1.start_ref), custom_call_target="tpu_custom_call" | custom-call | flops 4831838208 | bytes 2097152 | tf_op jit(solution)/shard_map/peer_tokens/pallas_call | solution.py:129
  14.6 27.0 %all_to_all.10 = f32[16,160,128]{2,1,0:T(8,128)S(1)} all-to-all(f32[16,160,128]{2,1,0:T(8,128)S(1)} %bitcast.3), channel_id=1, replica_groups={{0,16,1,17,2,18,3,19,4,20,5,21,6,22,7,23},{8,24,9,25,10,26,11,27,12,28,..., dimensions={0} | all-to-all | bytes 2621440 | tf_op jit(solution)/shard_map/all_to_all | solution.py:141
  41.6 0.1 reduce_sum.18
  41.7 13.0 %all_to_all.11 = f32[8,160,128]{2,1,0:T(8,128)S(1)} all-to-all(f32[8,160,128]{2,1,0:T(8,128)S(1)} %broadcast_in_dim.2), channel_id=1, replica_groups={{0,16,32,48,64,80,96,112},{1,17,33,49,65,81,97,113},{2,18,34,50,66,82,9..., dimensions={0} | all-to-all | bytes 1310720 | tf_op jit(solution)/shard_map/all_to_all | solution.py:146
  54.7 3.2 %collective-permute-start.2 = (f32[40,8,128]{2,1,0:T(8,128)S(1)}, f32[40,8,128]{2,1,0:T(8,128)S(1)}, u32[]{:S(2)}, u32[]{:S(2)}) collective-permute-start(f32[40,8,128]{2,1,0:T(8,128)S(1)} %reduce_sum.19.mine_ref), channel_id=1, source_target_pairs={{0,8},{1,9},{2,10},{3,11},{4,12},{5,13},{6,14},{7,15},{8,0},{9,1},... | collective-permute-start | bytes 491528 | tf_op jit(solution)/shard_map/ppermute | solution.py:148
  57.9 1.0 %collective-permute-done.2.other_ref = f32[40,8,128]{2,1,0:T(8,128)S(1)} collective-permute-done((f32[40,8,128]{2,1,0:T(8,128)S(1)}, f32[40,8,128]{2,1,0:T(8,128)S(1)}, u32[]{:S(2)}, u32[]{:S(2)}) %collective-permute-start.2) | collective-permute-done | bytes 163872 | tf_op jit(solution)/shard_map/ppermute | solution.py:148
  58.9 0.9 %lift.1 = f32[4,48,384]{2,1,0:T(8,128)} custom-call(s32[1]{0:T(128)} %bitcast.core_ref, f32[40,8,128]{2,1,0:T(8,128)S(1)} %reduce_sum.19.mine_ref, f32[40,8,128]{2,1,0:T(8,128)S(1)} %collective-permute-done.2.other_ref), custom_call_target="tpu_custom_call" | custom-call | tf_op jit(solution)/shard_map/lift/pallas_call | solution.py:149
  (2 shorter events, 0.1 us)
Async XLA Ops:
  0.0 8.6 %collective-permute-start.1 = (s32[5,8,8192]{2,1,0:T(8,128)}, s32[5,8,8192]{2,1,0:T(8,128)S(1)}, u32[]{:S(2)}, u32[]{:S(2)}) collective-permute-start(s32[5,8,8192]{2,1,0:T(8,128)} %ids_ref.1), channel_id=1, source_target_pairs={{0,8},{1,9},{2,10},{3,11},{4,12},{5,13},{6,14},{7,15},{8,0},{9,1},... | collective-permute-start | bytes 3932168 | tf_op jit(solution)/shard_map/ppermute | solution.py:111
  1.4 7.2 %collective-permute-start = (s32[1]{0:T(128)}, s32[1]{0:T(128)}, u32[]{:S(2)}, u32[]{:S(2)}) collective-permute-start(s32[1]{0:T(128)} %param.3), channel_id=1, source_target_pairs={{0,8},{1,9},{2,10},{3,11},{4,12},{5,13},{6,14},{7,15},{8,0},{9,1},... | collective-permute-start | bytes 20 | tf_op jit(solution)/shard_map/ppermute | solution.py:112
  2.0 1.3 %copy-start = (s32[5,8,8192]{2,1,0:T(8,128)S(1)}, s32[5,8,8192]{2,1,0:T(8,128)}, u32[]{:S(2)}) copy-start(s32[5,8,8192]{2,1,0:T(8,128)} %ids_ref.1) | copy-start | bytes 3932164
  54.7 4.2 %collective-permute-start.2 = (f32[40,8,128]{2,1,0:T(8,128)S(1)}, f32[40,8,128]{2,1,0:T(8,128)S(1)}, u32[]{:S(2)}, u32[]{:S(2)}) collective-permute-start(f32[40,8,128]{2,1,0:T(8,128)S(1)} %reduce_sum.19.mine_ref), channel_id=1, source_target_pairs={{0,8},{1,9},{2,10},{3,11},{4,12},{5,13},{6,14},{7,15},{8,0},{9,1},... | collective-permute-start | bytes 491528 | tf_op jit(solution)/shard_map/ppermute | solution.py:148
